TPU v7x, 16 devices: a 4x2x1 block of a 4x4x8 slice. The times are simulated.
16 devices in a mesh: data: 2 (over y, z), seq: 8 (over x, core).
Axes of the slice: x: 4, y: 2, z: 1, core: 2. Of those that a mesh axis runs over, the one named last changes fastest.
The devices are a block of a 4x4x8 slice.
Arguments:
- act_in: bfloat16 [8, 2048, 1024], P('data', 'seq'), parts along dimension 0
- ln1_scale: float32 [1024], replicated
- ln1_bias: float32 [1024], replicated
- w_in: bfloat16 [1024, 4096], replicated
- b_in: float32 [4096], replicated
- ln2_scale: float32 [2048], replicated
- ln2_bias: float32 [2048], replicated
- w_spatial: bfloat16 [2048, 2048], replicated
- b_spatial: float32 [2048], replicated
- causal_mask: int32 [2048, 2048], replicated
- w_out: bfloat16 [2048, 1024], replicated
- b_out: float32 [1024], replicated
Outputs:
- output: bfloat16 [8, 2048, 1024], P('data', 'seq'), parts along dimension 0
There are 2 independent parts. A program takes and returns all parts, laid end to end along the dimension named above; an argument that names none is the same for every part.
All inputs are finite; a program needn't handle non-finite values.
Results may differ from a plain program's by a relative error of at most 0.0115268.
Values are sent between devices in bfloat16 or wider.
A program may use at most 768 MiB of HBM per device.

v0:
```python
import jax
import jax.numpy as jnp
from jax import lax
from jax.sharding import PartitionSpec as P

LN_EPS = 1e-6


def layer_norm(features, ln_gain, ln_shift):
    mean_val = jnp.mean(features, axis=-1, keepdims=True)
    centered = features - mean_val
    var_val = jnp.mean(centered * centered, axis=-1, keepdims=True)
    return centered * lax.rsqrt(var_val + LN_EPS) * ln_gain + ln_shift


def solution(mesh):
    row_spec = P('data', 'seq', None)
    replicated = P()

    def local_block(act_in, ln1_scale, ln1_bias, w_in, b_in, ln2_scale, ln2_bias, w_spatial, b_spatial, causal_mask, w_out, b_out):
        gate_dim = w_out.shape[0]
        normed = layer_norm(act_in.astype(jnp.float32), ln1_scale, ln1_bias).astype(jnp.bfloat16)
        hidden = jax.nn.gelu(jnp.einsum('bsd,df->bsf', normed, w_in, preferred_element_type=jnp.float32) + b_in, approximate=True).astype(jnp.bfloat16)
        gate_half = hidden[:, :, :gate_dim]
        value_norm = layer_norm(hidden[:, :, gate_dim:].astype(jnp.float32), ln2_scale, ln2_bias).astype(jnp.bfloat16)
        value_cols = lax.all_to_all(value_norm, 'seq', 2, 1, tiled=True)
        w_masked = jnp.where(causal_mask > 0, w_spatial, jnp.zeros_like(w_spatial))
        spatial_cols = (jnp.einsum('ij,bjc->bic', w_masked, value_cols, preferred_element_type=jnp.float32) + b_spatial[None, :, None]).astype(jnp.bfloat16)
        spatial_rows = lax.all_to_all(spatial_cols, 'seq', 1, 2, tiled=True)
        gated_act = (gate_half.astype(jnp.float32) * spatial_rows.astype(jnp.float32)).astype(jnp.bfloat16)
        projected = jnp.einsum('bsc,cd->bsd', gated_act, w_out, preferred_element_type=jnp.float32) + b_out
        return (act_in.astype(jnp.float32) + projected).astype(jnp.bfloat16)

    return jax.shard_map(local_block, mesh=mesh, in_specs=(row_spec,) + (replicated,) * 11, out_specs=row_spec, check_vma=False)
```

profile of v0, /device:TPU:112, one launch (start us, length us, event | category | flops | bytes accessed | tf_op | source)
XLA Modules:
  0.0 205.1 jit_solution(12417362373088614365)
XLA Ops:
  0.0 1.9 convert_reduce_fusion.1
  1.9 2.3 %fusion.24 = f32[4,256]{1,0:T(4,128)S(1)} fusion(bf16[4,256,1024]{2,1,0:T(8,128)(2,1)} %param.12, f32[4,256]{1,0:T(4,128)S(1)} %broadcast_multiply_fusion.1), kind=kLoop, calls=%fused_computation.31 | loop fusion | flops 4193280 | bytes 2105344 | tf_op jit(solution)/shard_map/reduce_sum | solution.py:12
  4.2 16.7 %fusion.7 = bf16[4,256,4096]{2,1,0:T(8,128)(2,1)S(1)} fusion(f32[4096]{0:T(1024)} %param.16, bf16[1024,4096]{1,0:T(8,128)(2,1)} %param.15, bf16[4,256,1024]{2,1,0:T(8,128)(2,1)} %param.12, f32[1024]{0:T(1024)} %param.14, f32[1024]{0:T(1024)} %param.13, f32[4,256]{1,0:T(4,128)S(1)} %add_rsqrt_fusion.1, f32[4,256]{1,0:T(4,128)S(1)} %broadcast_multiply_fusion.1), kind=kOutput, calls=%fused_computation.8 | convolution fusion | flops 8638169088 | bytes 18907136 | tf_op jit(solution)/shard_map/bsd,df->bsf/dot_general | solution.py:23
  21.0 0.0 copy-start
  21.0 0.0 copy-start.2
  21.0 0.0 copy-start.3
  21.0 0.6 convert_reduce_fusion
  21.6 1.4 fusion.10
  23.0 1.2 copy-done
  24.2 0.0 copy-done.2
  24.2 0.0 copy-done.3
  24.2 3.0 %fusion.13 = bf16[4,256,2048]{2,1,0:T(8,128)(2,1)} fusion(f32[2048]{0:T(1024)S(1)} %copy-done.2, f32[2048]{0:T(1024)S(1)} %copy-done.3, f32[4,256]{1,0:T(4,128)S(1)} %add_rsqrt_fusion, f32[4,256]{1,0:T(4,128)S(1)} %broadcast_multiply_fusion, bf16[4,256,4096]{2,1,0:T(8,128)(2,1)S(1)} %fusion.7), kind=kLoop, calls=%fused_computation.17 | loop fusion | flops 12582912 | bytes 8413184 | tf_op jit(solution)/shard_map/convert_element_type | solution.py:25
  27.2 7.5 %copy.15 = bf16[4,256,2048]{1,0,2:T(4,128)(2,1)} copy(bf16[4,256,2048]{2,1,0:T(8,128)(2,1)} %fusion.13) | data formatting | bytes 8388608 | tf_op jit(solution)/shard_map/convert_element_type | solution.py:25
  34.7 54.9 %all_to_all.27 = bf16[4,256,2048]{1,0,2:T(4,128)(2,1)S(1)} all-to-all(bf16[4,256,2048]{1,0,2:T(4,128)(2,1)} %copy.15), channel_id=1, replica_groups=mesh['data'=2,'seq'=8] {'seq'}, dimensions={2} | all-to-all | bytes 8388608 | tf_op jit(solution)/shard_map/all_to_all | solution.py:26
  89.5 0.0 copy-start.4
  89.5 4.4 %copy.22 = bf16[4,256,8,256]{1,2,3,0:T(8,128)(2,1)} copy(bf16[4,256,8,256]{1,0,3,2:T(4,128)(2,1)S(1)} %bitcast.35) | data formatting | bytes 8388608 | tf_op jit(solution)/shard_map/all_to_all | solution.py:26
  93.9 7.4 %all_to_all.23 = bf16[4,2048,256]{1,2,0:T(8,128)(2,1)} reshape(bf16[4,8,256,256]{2,1,3,0:T(8,128)(2,1)} %bitcast.36) | data formatting | bytes 8388608 | tf_op jit(solution)/shard_map/all_to_all | solution.py:26
  101.3 0.0 copy-done.4
  101.3 16.3 %fusion.29 = bf16[4,2048,256]{1,2,0:T(8,128)(2,1)} fusion(f32[2048]{0:T(1024)S(1)} %copy-done.4, bf16[4,2048,256]{1,2,0:T(8,128)(2,1)} %all_to_all.23, bf16[2048,2048]{1,0:T(8,128)(2,1)} %param.19, s32[2048,2048]{1,0:T(8,128)} %param.21), kind=kOutput, calls=%fused_computation.36 | convolution fusion | flops 8602517504 | bytes 33562624 | tf_op jit(solution)/shard_map/ij,bjc->bic/dot_general | solution.py:28
  117.6 7.5 %copy.17 = bf16[4,2048,256]{2,0,1:T(4,128)(2,1)} copy(bf16[4,2048,256]{1,2,0:T(8,128)(2,1)} %fusion.29) | data formatting | bytes 8388608 | tf_op jit(solution)/shard_map/convert_element_type | solution.py:28
  125.1 53.3 %all_to_all.28 = bf16[4,2048,256]{2,0,1:T(4,128)(2,1)S(1)} all-to-all(bf16[4,2048,256]{2,0,1:T(4,128)(2,1)} %copy.17), channel_id=1, replica_groups=mesh['data'=2,'seq'=8] {'seq'}, dimensions={1} | all-to-all | bytes 8388608 | tf_op jit(solution)/shard_map/all_to_all | solution.py:29
  178.4 5.7 %copy.21 = f32[4,8,256,256]{3,1,2,0:T(8,128)} copy(bf16[4,8,256,256]{3,0,2,1:T(4,128)(2,1)S(1)} %bitcast.34) | data formatting | bytes 12582912 | tf_op jit(solution)/shard_map/convert_element_type | solution.py:30
  184.0 0.0 copy-start.1
  184.0 0.0 copy-start.5
  184.0 9.4 %reshape.35 = f32[4,256,2048]{2,1,0:T(8,128)} reshape(f32[4,256,8,256]{3,2,1,0:T(8,128)} %bitcast.33) | data formatting | bytes 16777216 | tf_op jit(solution)/shard_map/convert_element_type | solution.py:30
  193.4 0.0 copy-done.1
  193.4 0.0 copy-done.5
  193.4 11.7 %fusion.28 = bf16[4,256,1024]{2,1,0:T(8,128)(2,1)} fusion(bf16[4,256,1024]{2,1,0:T(8,128)(2,1)S(1)} %copy-done.1, f32[1024]{0:T(1024)S(1)} %copy-done.5, bf16[2048,1024]{1,0:T(8,128)(2,1)} %param.22, f32[4,256,2048]{2,1,0:T(8,128)} %reshape.35, bf16[4,256,4096]{2,1,0:T(8,128)(2,1)} %copy-done), kind=kOutput, calls=%fused_computation.35 | convolution fusion | flops 4305453056 | bytes 20975616 | tf_op jit(solution)/shard_map/bsc,cd->bsd/dot_general | solution.py:31
  (4 shorter events, 0.0 us)
Async XLA Ops:
  21.0 3.2 %copy-start = (bf16[4,256,4096]{2,1,0:T(8,128)(2,1)}, bf16[4,256,4096]{2,1,0:T(8,128)(2,1)S(1)}, u32[]{:S(2)}) copy-start(bf16[4,256,4096]{2,1,0:T(8,128)(2,1)S(1)} %fusion.7) | copy-start | bytes 25165828
  21.0 3.2 %copy-start.2 = (f32[2048]{0:T(1024)S(1)}, f32[2048]{0:T(1024)}, u32[]{:S(2)}) copy-start(f32[2048]{0:T(1024)} %param.18) | copy-start | bytes 24580
  21.0 3.2 %copy-start.3 = (f32[2048]{0:T(1024)S(1)}, f32[2048]{0:T(1024)}, u32[]{:S(2)}) copy-start(f32[2048]{0:T(1024)} %param.17) | copy-start | bytes 24580
  89.5 11.8 %copy-start.4 = (f32[2048]{0:T(1024)S(1)}, f32[2048]{0:T(1024)}, u32[]{:S(2)}) copy-start(f32[2048]{0:T(1024)} %param.20) | copy-start | bytes 24580
  184.0 9.4 %copy-start.1 = (bf16[4,256,1024]{2,1,0:T(8,128)(2,1)S(1)}, bf16[4,256,1024]{2,1,0:T(8,128)(2,1)}, u32[]{:S(2)}) copy-start(bf16[4,256,1024]{2,1,0:T(8,128)(2,1)} %param.12) | copy-start | bytes 6291460
  184.0 9.4 %copy-start.5 = (f32[1024]{0:T(1024)S(1)}, f32[1024]{0:T(1024)}, u32[]{:S(2)}) copy-start(f32[1024]{0:T(1024)} %param.23) | copy-start | bytes 12292
where the time goes:
time: 206 us; the launch traced here: 205 us
  blocking collectives  108 us (52%)
  matrix products  44.7 us (22%)
  local copies, waits for them, and re-layouts  43 us (21%)
  other arithmetic  9.25 us (4%)
    all_to_all x1, blocking collectives, local_block(): value_cols = lax.all_to_all(value_norm, 'seq', 2, 1, tiled=True)  54.9 us
    all_to_all x1, blocking collectives, local_block(): spatial_rows = lax.all_to_all(spatial_cols, 'seq', 1, 2, tiled=True)  53.3 us
    dot_general x1, matrix products, local_block(): jnp.einsum('bsd,df->bsf', normed, w_in, preferred_element_type=jnp.float32)  16.7 us
    dot_general x1, matrix products, local_block(): jnp.einsum('ij,bjc->bic', w_masked, value_cols, preferred_element_type=jn...  16.3 us
    convert_element_type x2, local copies, waits for them, and re-layouts, local_block(): spatial_rows.astype(jnp.float32)  15.1 us
    all_to_all x2, local copies, waits for them, and re-layouts, local_block(): value_cols = lax.all_to_all(value_norm, 'seq', 2, 1, tiled=True)  11.8 us
    dot_general x1, matrix products, local_block(): jnp.einsum('bsc,cd->bsd', gated_act, w_out, preferred_element_type=jnp.fl...  11.7 us
    convert_element_type x1, local copies, waits for them, and re-layouts, local_block(): (jnp.einsum('ij,bjc->bic', w_masked, value_cols, preferred_element_type=j...  7.48 us

commit v1 on v0

v1 whole, which is shorter than its diff:
```python
import functools

import jax
import jax.numpy as jnp
from jax import lax
from jax.experimental import pallas as pl
from jax.experimental.pallas import tpu as pltpu
from jax.sharding import PartitionSpec as P

LN_EPS = 1e-6
MESH = pl.DeviceIdType.MESH
F32 = jnp.float32
BF16 = jnp.bfloat16

V, W, O, M = 0, 4, 8, 12
SCHEDULES = (
    (V + 0, M, V + 1, W + 0, W + 1, O + 1, V + 3, V + 2, W + 2, O + 2, W + 3, O + 3, O + 0),
    (V + 1, M, V + 0, W + 0, O + 0, V + 2, W + 1, W + 2, O + 2, V + 3, W + 3, O + 3, O + 1),
    (V + 2, M, V + 0, W + 0, O + 0, V + 1, W + 1, O + 1, V + 3, W + 2, W + 3, O + 3, O + 2),
    (V + 3, M, V + 0, W + 0, O + 0, V + 2, V + 1, W + 1, O + 1, W + 2, O + 2, W + 3, O + 3),
)
HALF = 7


def pack(steps):
    return sum(s << (4 * i) for i, s in enumerate(steps))


def layer_norm_rows(rows, gain, shift):
    mean = jnp.mean(rows, axis=-1, keepdims=True)
    centered = rows - mean
    var = jnp.mean(centered * centered, axis=-1, keepdims=True)
    return centered * lax.rsqrt(var + LN_EPS) * gain + shift


def gelu(a):
    c0 = 0.7978845608028654
    inner = a * (c0 + (c0 * 0.044715) * (a * a))
    return a * (0.5 + 0.5 * jnp.tanh(inner))


def kernel(cores, x_ref, ln1s_h, ln1b_h, win_h, bin_h, ln2s_h, ln2b_h, wsp_h, bsp_h, mask_h, wout_h, bout_h, out_ref,
           xbuf, u, h, vn, wm, mask, win, wout, q, obuf, ln1s, ln1b, b_in, ln2s, ln2b, bsp, bout,
           small_sem, win_sem, wout_sem, wsp_sem, mask_sem, xs_sem, xr_sem, vs_sem, vr_sem, os_sem, or_sem):
    data, me = lax.axis_index("data"), lax.axis_index("seq")
    chip, core = me // cores, me % cores
    partner = (data, chip * cores + (cores - 1 - core))
    chips, rows, width = x_ref.shape
    gate = wout_h.shape[0]

    def block_of(k):
        return k * cores + core

    def row_slice(k):
        return pl.ds(pl.multiple_of(block_of(k) * rows, rows), rows)

    own = pltpu.make_async_copy(x_ref.at[chip], xbuf.at[chip], xr_sem.at[chip])
    own.start()
    smalls = [pltpu.make_async_copy(src, dst, small_sem.at[i]) for i, (src, dst) in enumerate(
        ((ln1s_h, ln1s), (ln1b_h, ln1b), (bin_h, b_in), (ln2s_h, ln2s), (ln2b_h, ln2b), (bsp_h, bsp), (bout_h, bout)))]
    for cp in smalls:
        cp.start()
    win_v = pltpu.make_async_copy(win_h.at[:, pl.ds(gate, gate)], win.at[:, pl.ds(gate, gate)], win_sem.at[0])
    win_g = pltpu.make_async_copy(win_h.at[:, pl.ds(0, gate)], win.at[:, pl.ds(0, gate)], win_sem.at[1])
    win_v.start()

    barrier = pltpu.get_barrier_semaphore()
    pl.semaphore_signal(barrier, inc=1, device_id=partner, device_id_type=MESH)
    for d in range(1, chips):
        pl.semaphore_signal(barrier, inc=1, device_id=(data, (chip + d) % chips * cores + core), device_id_type=MESH)
    pl.semaphore_wait(barrier, chips)

    def send_x(d):
        to = (chip + d) % chips
        pltpu.make_async_remote_copy(
            src_ref=x_ref.at[to], dst_ref=xbuf.at[chip], send_sem=xs_sem.at[d - 1], recv_sem=xr_sem.at[chip],
            device_id=(data, to * cores + core), device_id_type=MESH).start()

    @pl.when(chip == 0)
    def _():
        send_x(chips // 2)

    for d in range(1, chips):
        if d != chips // 2:
            send_x(d)

    @pl.when(chip != 0)
    def _():
        send_x(chips // 2)

    win_g.start()
    spatial_loads = []
    for k in range(chips):
        cols = pl.ds(0, (k + 1) * cores * rows)
        a = pltpu.make_async_copy(wsp_h.at[row_slice(k), cols], wm.at[k, :, cols], wsp_sem.at[k])
        b = pltpu.make_async_copy(mask_h.at[row_slice(k), cols], mask.at[k, :, cols], mask_sem.at[k])
        a.start()
        b.start()
        spatial_loads += [a, b]
    wout_load = pltpu.make_async_copy(wout_h, wout, wout_sem)
    wout_load.start()

    def dense_tiles(k, first, count, tile):
        def body(t, carry):
            cols = pl.ds(pl.multiple_of(first + t * tile, tile), tile)
            a = jnp.dot(u[...], win[:, cols], preferred_element_type=F32) + b_in[:, cols]
            h[k, :, cols] = gelu(a).astype(BF16)
            return carry
        lax.fori_loop(0, count, body, 0)

    def vn_copy(k):
        return pltpu.make_async_remote_copy(
            src_ref=vn.at[row_slice(k), :], dst_ref=vn.at[row_slice(k), :], send_sem=vs_sem.at[k], recv_sem=vr_sem.at[k],
            device_id=partner, device_id_type=MESH)

    def do_v(k):
        pltpu.make_async_copy(xbuf.at[k], xbuf.at[k], xr_sem.at[k]).wait()

        @pl.when(k == chip)
        def _():
            for cp in smalls:
                cp.wait()

        chunk = 32

        def ln1_body(r, carry):
            rs = pl.ds(pl.multiple_of(r * chunk, chunk), chunk)
            u[rs, :] = layer_norm_rows(xbuf[k, rs, :].astype(F32), ln1s[...], ln1b[...]).astype(BF16)
            return carry
        lax.fori_loop(0, rows // chunk, ln1_body, 0, unroll=2)

        @pl.when(k == chip)
        def _():
            win_v.wait()
        tile = gate // 4
        dense_tiles(k, gate, 4, tile)
        chunk2 = 16
        base = block_of(k) * rows

        def ln2_body(r, carry):
            rs = pl.ds(pl.multiple_of(r * chunk2, chunk2), chunk2)
            ws = pl.ds(pl.multiple_of(base + r * chunk2, chunk2), chunk2)
            vn[ws, :] = layer_norm_rows(h[k, rs, gate:].astype(F32), ln2s[...], ln2b[...]).astype(BF16)
            return carry
        lax.fori_loop(0, rows // chunk2, ln2_body, 0, unroll=2)
        vn_copy(k).start()

        @pl.when(k == chip)
        def _():
            win_g.wait()
        dense_tiles(k, 0, 4, tile)

    def do_mask():
        for cp in spatial_loads:
            cp.wait()
        chunk = 32
        for k in range(chips):
            cols = slice(0, (k + 1) * cores * rows)

            def body(r, carry):
                rs = pl.ds(pl.multiple_of(r * chunk, chunk), chunk)
                keep = mask[k, rs, cols] > 0
                wm[k, rs, cols] = jnp.where(keep, wm[k, rs, cols].astype(F32), 0.0).astype(BF16)
                return carry
            lax.fori_loop(0, rows // chunk, body, 0)
        wout_load.wait()

    def do_o(k):
        bias_row = bsp[:, row_slice(k)]
        bias = jnp.transpose(jnp.broadcast_to(bias_row, (128, rows)))[:, :1]
        for kk in range(chips):
            @pl.when(k == kk)
            def _():
                depth = (kk + 1) * cores * rows
                tile = gate // 4

                def body(t, carry):
                    cols = pl.ds(pl.multiple_of(t * tile, tile), tile)
                    s = jnp.dot(wm[kk, :, :depth], vn[:depth, cols], preferred_element_type=F32) + bias
                    q[:, cols] = (h[kk, :, cols].astype(F32) * s.astype(BF16).astype(F32)).astype(BF16)
                    return carry
                lax.fori_loop(0, gate // tile, body, 0)
        tile = width // 2

        def out_body(t, carry):
            cols = pl.ds(pl.multiple_of(t * tile, tile), tile)
            y = jnp.dot(q[...], wout[:, cols], preferred_element_type=F32) + bout[:, cols]
            obuf[k, :, cols] = (xbuf[k, :, cols].astype(F32) + y).astype(BF16)
            return carry
        lax.fori_loop(0, width // tile, out_body, 0)

        @pl.when(k == chip)
        def _():
            pltpu.make_async_copy(obuf.at[k], out_ref.at[chip], or_sem.at[chip]).start()

        @pl.when(k != chip)
        def _():
            out_copy(k).start()

    def out_copy(k):
        return pltpu.make_async_remote_copy(
            src_ref=obuf.at[k], dst_ref=out_ref.at[chip], send_sem=os_sem.at[k], recv_sem=or_sem.at[chip],
            device_id=(data, k * cores + core), device_id_type=MESH)

    low = high = jnp.int32(0)
    for c, steps in enumerate(SCHEDULES):
        low = jnp.where(chip == c, pack(steps[:HALF]), low)
        high = jnp.where(chip == c, pack(steps[HALF:]), high)

    def step(i, carry):
        code = jnp.where(i < HALF, low, high)
        action = lax.shift_right_logical(code, 4 * (i % HALF)) % 16
        k = action % 4

        @pl.when(action // 4 == V // 4)
        def _():
            do_v(k)

        @pl.when(action // 4 == W // 4)
        def _():
            vn_copy(k).wait_recv()

        @pl.when(action // 4 == O // 4)
        def _():
            do_o(k)

        @pl.when(action // 4 == M // 4)
        def _():
            do_mask()
        return carry
    lax.fori_loop(0, len(SCHEDULES[0]), step, 0)

    for d in range(1, chips):
        to = (chip + d) % chips
        pltpu.make_async_remote_copy(
            src_ref=x_ref.at[to], dst_ref=xbuf.at[chip], send_sem=xs_sem.at[d - 1], recv_sem=xr_sem.at[chip],
            device_id=(data, to * cores + core), device_id_type=MESH).wait_send()
    for k in range(chips):
        vn_copy(k).wait_send()

        @pl.when(k != chip)
        def _():
            out_copy(k).wait_send()
    for k in range(chips):
        pltpu.make_async_copy(out_ref.at[k], out_ref.at[k], or_sem.at[k]).wait()


def solution(mesh):
    row_spec = P('data', 'seq', None)
    replicated = P()

    def local_block(act_in, ln1_scale, ln1_bias, w_in, b_in, ln2_scale, ln2_bias, w_spatial, b_spatial, causal_mask, w_out, b_out):
        chips, rows, width = act_in.shape
        cores = mesh.shape['seq'] // chips
        ffn, gate, total = w_in.shape[1], w_out.shape[0], w_spatial.shape[0]
        any_spec = pl.BlockSpec(memory_space=pl.ANY)
        row = lambda a: a.reshape(1, -1)
        dma = pltpu.SemaphoreType.DMA
        return pl.pallas_call(
            functools.partial(kernel, cores),
            out_shape=jax.ShapeDtypeStruct(act_in.shape, act_in.dtype),
            in_specs=[any_spec] * 12,
            out_specs=any_spec,
            scratch_shapes=[
                pltpu.VMEM((chips, rows, width), BF16),
                pltpu.VMEM((rows, width), BF16),
                pltpu.VMEM((chips, rows, ffn), BF16),
                pltpu.VMEM((total, gate), BF16),
                pltpu.VMEM((chips, rows, total), BF16),
                pltpu.VMEM((chips, rows, total), jnp.int32),
                pltpu.VMEM((width, ffn), BF16),
                pltpu.VMEM((gate, width), BF16),
                pltpu.VMEM((rows, gate), BF16),
                pltpu.VMEM((chips, rows, width), BF16),
                pltpu.VMEM((1, width), F32),
                pltpu.VMEM((1, width), F32),
                pltpu.VMEM((1, ffn), F32),
                pltpu.VMEM((1, gate), F32),
                pltpu.VMEM((1, gate), F32),
                pltpu.VMEM((1, total), F32),
                pltpu.VMEM((1, width), F32),
                dma((7,)), dma((2,)), dma, dma((chips,)), dma((chips,)),
                dma((chips - 1,)), dma((chips,)), dma((chips,)), dma((chips,)), dma((chips,)), dma((chips,)),
            ],
            compiler_params=pltpu.CompilerParams(collective_id=0, has_side_effects=True, vmem_limit_bytes=66_000_000),
        )(act_in, row(ln1_scale), row(ln1_bias), w_in, row(b_in), row(ln2_scale), row(ln2_bias), w_spatial, row(b_spatial),
          causal_mask, w_out, row(b_out))

    return jax.shard_map(local_block, mesh=mesh, in_specs=(row_spec,) + (replicated,) * 11, out_specs=row_spec, check_vma=False)
```

time: 206 us -> 77.8 us (0.38)
  blocking collectives: 108 us -> 0 us
  Pallas kernels: 0 us -> 74.6 us
  matrix products: 44.7 us -> 0 us
  local copies, waits for them, and re-layouts: 43 us -> 3.08 us
  other arithmetic: 9.25 us -> 0 us
    all_to_all x2 -> x0, blocking collectives: 108 us -> none  [the longest x1 54.9 us: local_block(): value_cols = lax.all_to_all(value_norm, 'seq', 2, 1, tiled=True)]
    pallas_call x0 -> x1, Pallas kernels: none -> 74.6 us  [local_block(): pl.pallas_call(functools.partial(kernel, cores), out_shape=jax.ShapeDtype...]
    dot_general x3 -> x0, matrix products: 44.7 us -> none  [the longest x1 16.7 us: local_block(): jnp.einsum('bsd,df->bsf', normed, w_in, preferred_element_type=jnp.float32)]
    convert_element_type x4 -> x0, local copies, waits for them, and re-layouts: 30 us -> none  [the longest x2 15.1 us: local_block(): spatial_rows.astype(jnp.float32)]
    all_to_all x2 -> x0, local copies, waits for them, and re-layouts: 11.8 us -> none  [local_block(): value_cols = lax.all_to_all(value_norm, 'seq', 2, 1, tiled=True)]
    reduce_sum x4 -> x0, other arithmetic: 6.22 us -> none  [the longest x2 3.66 us: layer_norm(): var_val = jnp.mean(centered * centered, axis=-1, keepdims=True)]
    convert_element_type x1 -> x0, other arithmetic: 3 us -> none  [local_block(): layer_norm(hidden[:, :, gate_dim:].astype(jnp.float32), ln2_scale, ln2_bias)]
where the time goes in v1:
time: 77.8 us; the launch traced here: 77.7 us
  Pallas kernels  74.6 us (96%)
  local copies, waits for them, and re-layouts  3.08 us (4%)
    pallas_call x1, Pallas kernels, local_block(): pl.pallas_call(functools.partial(kernel, cores), out_shape=jax.ShapeDtype...  74.6 us
    unnamed x1, local copies, waits for them, and re-layouts  3.08 us

profile of v1, /device:TPU:112, one launch (start us, length us, event | category | flops | bytes accessed | tf_op | source)
XLA Modules:
  0.0 77.7 jit_solution(3701314059159153429)
XLA Ops:
  0.0 74.6 %shard_map.118 = bf16[4,256,1024]{2,1,0:T(8,128)(2,1)} custom-call(bf16[4,256,1024]{2,1,0:T(8,128)(2,1)} %x_ref.1, f32[1,1024]{1,0:T(1,128)} %bitcast.11, f32[1,1024]{1,0:T(1,128)} %bitcast.12, bf16[1024,4096]{1,0:T(8,128)(2,1)} %win_h.1, f32[1,4096]{1,0:T(1,128)} %bitcast.7, f32[1,2048]{1,0:T(1,128)} %bitcast.8, f32[1,2048]{1,0:T(1,128)} %bitcast.9, ...), custom_call_target="tpu_custom_call" | custom-call | tf_op jit(solution)/shard_map/pallas_call | solution.py:259
  74.6 3.1 %copy.14 = bf16[4,256,1024]{2,1,0:T(8,128)(2,1)} copy(bf16[4,256,1024]{2,1,0:T(8,128)(2,1)} %shard_map.118) | data formatting | bytes 4194304

commit v2 on v1

--- a/solution.py
+++ b/solution.py
@@ -14,10 +14,10 @@
 
 V, W, O, M = 0, 4, 8, 12
 SCHEDULES = (
-    (V + 0, M, V + 1, W + 0, W + 1, O + 1, V + 3, V + 2, W + 2, O + 2, W + 3, O + 3, O + 0),
-    (V + 1, M, V + 0, W + 0, O + 0, V + 2, W + 1, W + 2, O + 2, V + 3, W + 3, O + 3, O + 1),
-    (V + 2, M, V + 0, W + 0, O + 0, V + 1, W + 1, O + 1, V + 3, W + 2, W + 3, O + 3, O + 2),
-    (V + 3, M, V + 0, W + 0, O + 0, V + 2, V + 1, W + 1, O + 1, W + 2, O + 2, W + 3, O + 3),
+    (V + 0, M, V + 1, V + 3, W + 0, W + 1, O + 1, V + 2, W + 2, O + 2, W + 3, O + 3, O + 0),
+    (V + 1, M, V + 0, V + 2, W + 0, O + 0, V + 3, W + 1, W + 2, O + 2, W + 3, O + 3, O + 1),
+    (V + 2, M, V + 1, V + 3, V + 0, W + 0, O + 0, W + 1, O + 1, W + 2, W + 3, O + 3, O + 2),
+    (V + 3, M, V + 0, V + 2, W + 0, O + 0, V + 1, W + 1, O + 1, W + 2, O + 2, W + 3, O + 3),
 )
 HALF = 7
 
@@ -40,7 +40,7 @@
 
 
 def kernel(cores, x_ref, ln1s_h, ln1b_h, win_h, bin_h, ln2s_h, ln2b_h, wsp_h, bsp_h, mask_h, wout_h, bout_h, out_ref,
-           xbuf, u, h, vn, wm, mask, win, wout, q, obuf, ln1s, ln1b, b_in, ln2s, ln2b, bsp, bout,
+           xbuf, u, hv, g, vn, wm, mask, win, wout, q, obuf, ln1s, ln1b, b_in, ln2s, ln2b, bsp, bout,
            small_sem, win_sem, wout_sem, wsp_sem, mask_sem, xs_sem, xr_sem, vs_sem, vr_sem, os_sem, or_sem):
     data, me = lax.axis_index("data"), lax.axis_index("seq")
     chip, core = me // cores, me % cores
@@ -76,17 +76,8 @@
             src_ref=x_ref.at[to], dst_ref=xbuf.at[chip], send_sem=xs_sem.at[d - 1], recv_sem=xr_sem.at[chip],
             device_id=(data, to * cores + core), device_id_type=MESH).start()
 
-    @pl.when(chip == 0)
-    def _():
-        send_x(chips // 2)
-
-    for d in range(1, chips):
-        if d != chips // 2:
-            send_x(d)
-
-    @pl.when(chip != 0)
-    def _():
-        send_x(chips // 2)
+    for d in (*(d for d in range(1, chips) if d != chips // 2), chips // 2):
+        send_x(d)
 
     win_g.start()
     spatial_loads = []
@@ -100,13 +91,11 @@
     wout_load = pltpu.make_async_copy(wout_h, wout, wout_sem)
     wout_load.start()
 
-    def dense_tiles(k, first, count, tile):
-        def body(t, carry):
-            cols = pl.ds(pl.multiple_of(first + t * tile, tile), tile)
-            a = jnp.dot(u[...], win[:, cols], preferred_element_type=F32) + b_in[:, cols]
-            h[k, :, cols] = gelu(a).astype(BF16)
-            return carry
-        lax.fori_loop(0, count, body, 0)
+    tile = gate // 4
+
+    def dense(cols):
+        a = jnp.dot(u[...], win[:, cols], preferred_element_type=F32) + b_in[:, cols]
+        return gelu(a).astype(BF16)
 
     def vn_copy(k):
         return pltpu.make_async_remote_copy(
@@ -127,28 +116,36 @@
             rs = pl.ds(pl.multiple_of(r * chunk, chunk), chunk)
             u[rs, :] = layer_norm_rows(xbuf[k, rs, :].astype(F32), ln1s[...], ln1b[...]).astype(BF16)
             return carry
-        lax.fori_loop(0, rows // chunk, ln1_body, 0, unroll=2)
+        lax.fori_loop(0, rows // chunk, ln1_body, 0, unroll=4)
 
         @pl.when(k == chip)
         def _():
             win_v.wait()
-        tile = gate // 4
-        dense_tiles(k, gate, 4, tile)
+
+        def value_body(t, carry):
+            start = pl.multiple_of(t * tile, tile)
+            hv[:, pl.ds(start, tile)] = dense(pl.ds(gate + start, tile))
+            return carry
+        lax.fori_loop(0, gate // tile, value_body, 0, unroll=True)
+
+        @pl.when(k == chip)
+        def _():
+            win_g.wait()
         chunk2 = 16
         base = block_of(k) * rows
-
-        def ln2_body(r, carry):
-            rs = pl.ds(pl.multiple_of(r * chunk2, chunk2), chunk2)
-            ws = pl.ds(pl.multiple_of(base + r * chunk2, chunk2), chunk2)
-            vn[ws, :] = layer_norm_rows(h[k, rs, gate:].astype(F32), ln2s[...], ln2b[...]).astype(BF16)
-            return carry
-        lax.fori_loop(0, rows // chunk2, ln2_body, 0, unroll=2)
+        per_tile = rows // chunk2 // (gate // tile)
+
+        def gate_body(t, carry):
+            cols = pl.ds(pl.multiple_of(t * tile, tile), tile)
+            g[k, :, cols] = dense(cols)
+            for r in range(per_tile):
+                first = (t * per_tile + r) * chunk2
+                rs = pl.ds(pl.multiple_of(first, chunk2), chunk2)
+                ws = pl.ds(pl.multiple_of(base + first, chunk2), chunk2)
+                vn[ws, :] = layer_norm_rows(hv[rs, :].astype(F32), ln2s[...], ln2b[...]).astype(BF16)
+            return carry
+        lax.fori_loop(0, gate // tile, gate_body, 0, unroll=True)
         vn_copy(k).start()
-
-        @pl.when(k == chip)
-        def _():
-            win_g.wait()
-        dense_tiles(k, 0, 4, tile)
 
     def do_mask():
         for cp in spatial_loads:
@@ -172,22 +169,20 @@
             @pl.when(k == kk)
             def _():
                 depth = (kk + 1) * cores * rows
-                tile = gate // 4
-
                 def body(t, carry):
                     cols = pl.ds(pl.multiple_of(t * tile, tile), tile)
                     s = jnp.dot(wm[kk, :, :depth], vn[:depth, cols], preferred_element_type=F32) + bias
-                    q[:, cols] = (h[kk, :, cols].astype(F32) * s.astype(BF16).astype(F32)).astype(BF16)
+                    q[:, cols] = (g[kk, :, cols].astype(F32) * s.astype(BF16).astype(F32)).astype(BF16)
                     return carry
-                lax.fori_loop(0, gate // tile, body, 0)
-        tile = width // 2
+                lax.fori_loop(0, gate // tile, body, 0, unroll=True)
+        out_tile = width // 2
 
         def out_body(t, carry):
-            cols = pl.ds(pl.multiple_of(t * tile, tile), tile)
+            cols = pl.ds(pl.multiple_of(t * out_tile, out_tile), out_tile)
             y = jnp.dot(q[...], wout[:, cols], preferred_element_type=F32) + bout[:, cols]
             obuf[k, :, cols] = (xbuf[k, :, cols].astype(F32) + y).astype(BF16)
             return carry
-        lax.fori_loop(0, width // tile, out_body, 0)
+        lax.fori_loop(0, width // out_tile, out_body, 0, unroll=True)
 
         @pl.when(k == chip)
         def _():
@@ -264,7 +259,8 @@
             scratch_shapes=[
                 pltpu.VMEM((chips, rows, width), BF16),
                 pltpu.VMEM((rows, width), BF16),
-                pltpu.VMEM((chips, rows, ffn), BF16),
+                pltpu.VMEM((rows, gate), BF16),
+                pltpu.VMEM((chips, rows, gate), BF16),
                 pltpu.VMEM((total, gate), BF16),
                 pltpu.VMEM((chips, rows, total), BF16),
                 pltpu.VMEM((chips, rows, total), jnp.int32),

time: 77.8 us -> 67.4 us (0.87)
  Pallas kernels: 74.6 us -> 63.7 us
    pallas_call x1, Pallas kernels: 74.6 us -> 63.7 us  [local_block(): pl.pallas_call(functools.partial(kernel, cores), out_shape=jax.ShapeDtype...]
where the time goes in v2:
time: 67.4 us; the launch traced here: 66.8 us
  Pallas kernels  63.7 us (95%)
  local copies, waits for them, and re-layouts  3.08 us (5%)
    pallas_call x1, Pallas kernels, local_block(): pl.pallas_call(functools.partial(kernel, cores), out_shape=jax.ShapeDtype...  63.7 us
    unnamed x1, local copies, waits for them, and re-layouts  3.08 us

profile of v2, /device:TPU:112, one launch (start us, length us, event | category | flops | bytes accessed | tf_op | source)
XLA Modules:
  0.0 66.8 jit_solution(16246172492320537347)
XLA Ops:
  0.0 63.7 %shard_map.118 = bf16[4,256,1024]{2,1,0:T(8,128)(2,1)} custom-call(bf16[4,256,1024]{2,1,0:T(8,128)(2,1)} %x_ref.1, f32[1,1024]{1,0:T(1,128)} %bitcast.11, f32[1,1024]{1,0:T(1,128)} %bitcast.12, bf16[1024,4096]{1,0:T(8,128)(2,1)} %win_h.1, f32[1,4096]{1,0:T(1,128)} %bitcast.7, f32[1,2048]{1,0:T(1,128)} %bitcast.8, f32[1,2048]{1,0:T(1,128)} %bitcast.9, ...), custom_call_target="tpu_custom_call" | custom-call | tf_op jit(solution)/shard_map/pallas_call | solution.py:254
  63.7 3.1 %copy.14 = bf16[4,256,1024]{2,1,0:T(8,128)(2,1)} copy(bf16[4,256,1024]{2,1,0:T(8,128)(2,1)} %shard_map.118) | data formatting | bytes 4194304

commit v3 on v2

v3 whole, which is shorter than its diff:
```python
import functools

import jax
import jax.numpy as jnp
from jax import lax
from jax.experimental import pallas as pl
from jax.experimental.pallas import tpu as pltpu
from jax.sharding import PartitionSpec as P

LN_EPS = 1e-6
MESH = pl.DeviceIdType.MESH
F32 = jnp.float32
BF16 = jnp.bfloat16

HALVES = 2


def V(k, half):
    return k * HALVES + half


def O(k, half):
    return 12 + k * HALVES + half


W, O_FIRST, G, BITS, PER_WORD = 8, 12, 20, 5, 6
SCHEDULES = (
    (V(1, 0), V(3, 0), V(1, 1), V(3, 1), V(2, 0), W + 0, W + 1, O(1, 0), O(1, 1), V(2, 1), W + 2, W + 3,
     O(3, 0), O(3, 1), G, O(2, 0), O(2, 1), O(0, 0), O(0, 1)),
    (V(0, 0), V(2, 0), V(0, 1), V(2, 1), W + 0, W + 1, O(0, 0), O(0, 1), V(3, 0), W + 2, O(2, 0), O(2, 1), V(3, 1), W + 3,
     O(3, 0), G, O(3, 1), O(1, 0), O(1, 1)),
    (V(1, 0), V(3, 0), V(1, 1), V(3, 1), V(0, 0), V(0, 1), W + 0, W + 1, O(1, 0), O(0, 0), O(1, 1), G, O(0, 1), W + 2, W + 3,
     O(3, 0), O(3, 1), O(2, 0), O(2, 1)),
    (V(0, 0), V(2, 0), V(0, 1), V(2, 1), W + 0, O(0, 0), O(0, 1), V(1, 0), V(1, 1), W + 1, O(1, 0), W + 2, O(2, 0), G,
     O(1, 1), O(2, 1), W + 3, O(3, 0), O(3, 1)),
)


def pack(steps):
    return sum(s << (BITS * i) for i, s in enumerate(steps))


def layer_norm_rows(rows, gain, shift):
    mean = jnp.mean(rows, axis=-1, keepdims=True)
    centered = rows - mean
    var = jnp.mean(centered * centered, axis=-1, keepdims=True)
    return centered * lax.rsqrt(var + LN_EPS) * gain + shift


def gelu(a):
    c0 = 0.7978845608028654
    inner = a * (c0 + (c0 * 0.044715) * (a * a))
    return a * (0.5 + 0.5 * jnp.tanh(inner))


def kernel(cores, x_ref, ln1s_h, ln1b_h, win_h, bin_h, ln2s_h, ln2b_h, wsp_h, bsp_h, mask_h, wout_h, bout_h, out_ref,
           xbuf, u, hv, g, vn, wm, mask, win, wout, q, obuf, ln1s, ln1b, b_in, ln2s, ln2b, bsp, bout,
           small_sem, win_sem, wout_sem, wsp_sem, mask_sem, xs_sem, xr_sem, vs_sem, vr_sem, os_sem, or_sem):
    data, me = lax.axis_index("data"), lax.axis_index("seq")
    chip, core = me // cores, me % cores
    partner = (data, chip * cores + (cores - 1 - core))
    chips, rows, width = x_ref.shape
    gate = wout_h.shape[0]

    def block_of(k):
        return k * cores + core

    def row_slice(k):
        return pl.ds(pl.multiple_of(block_of(k) * rows, rows), rows)

    part = rows // HALVES

    def part_rows(half):
        return pl.ds(pl.multiple_of(half * part, part), part)

    for half in range(HALVES):
        rs = part_rows(half)
        pltpu.make_async_copy(x_ref.at[chip, rs], xbuf.at[chip, rs], xr_sem.at[chip * HALVES + half]).start()
    smalls = [pltpu.make_async_copy(src, dst, small_sem.at[i]) for i, (src, dst) in enumerate(
        ((ln1s_h, ln1s), (ln1b_h, ln1b), (bin_h, b_in), (ln2s_h, ln2s), (ln2b_h, ln2b), (bsp_h, bsp), (bout_h, bout)))]
    for cp in smalls:
        cp.start()
    win_v = pltpu.make_async_copy(win_h.at[:, pl.ds(gate, gate)], win.at[:, pl.ds(gate, gate)], win_sem.at[0])
    win_g = pltpu.make_async_copy(win_h.at[:, pl.ds(0, gate)], win.at[:, pl.ds(0, gate)], win_sem.at[1])
    win_v.start()
    win_g.start()

    barrier = pltpu.get_barrier_semaphore()
    pl.semaphore_signal(barrier, inc=1, device_id=partner, device_id_type=MESH)
    for d in range(1, chips):
        pl.semaphore_signal(barrier, inc=1, device_id=(data, (chip + d) % chips * cores + core), device_id_type=MESH)
    pl.semaphore_wait(barrier, chips)

    def x_copy(d, half):
        to = (chip + d) % chips
        rs = part_rows(half)
        return pltpu.make_async_remote_copy(
            src_ref=x_ref.at[to, rs], dst_ref=xbuf.at[chip, rs], send_sem=xs_sem.at[(d - 1) * HALVES + half],
            recv_sem=xr_sem.at[chip * HALVES + half], device_id=(data, to * cores + core), device_id_type=MESH)

    near = [d for d in range(1, chips) if d != chips // 2]
    for group in (near, [chips // 2]):
        for half in range(HALVES):
            for d in group:
                x_copy(d, half).start()

    spatial_loads = []
    for k in range(chips):
        cols = pl.ds(0, (k + 1) * cores * rows)
        spatial_loads += [
            pltpu.make_async_copy(wsp_h.at[row_slice(k), cols], wm.at[k, :, cols], wsp_sem.at[k]),
            pltpu.make_async_copy(mask_h.at[row_slice(k), cols], mask.at[k, :, cols], mask_sem.at[k]),
        ]
    wout_load = pltpu.make_async_copy(wout_h, wout, wout_sem)

    tile = gate // 4

    def dense(count, cols):
        a = jnp.dot(u[:count, :], win[:, cols], preferred_element_type=F32) + b_in[:, cols]
        return gelu(a).astype(BF16)

    def vn_copy(k, half):
        ws = pl.ds(pl.multiple_of(block_of(k) * rows + half * part, part), part)
        return pltpu.make_async_remote_copy(
            src_ref=vn.at[ws, :], dst_ref=vn.at[ws, :], send_sem=vs_sem.at[k * HALVES + half],
            recv_sem=vr_sem.at[k * HALVES + half], device_id=partner, device_id_type=MESH)

    def ln1(k, first, count):
        chunk = 32

        def body(r, carry):
            us = pl.ds(pl.multiple_of(r * chunk, chunk), chunk)
            xs = pl.ds(pl.multiple_of(first + r * chunk, chunk), chunk)
            u[us, :] = layer_norm_rows(xbuf[k, xs, :].astype(F32), ln1s[...], ln1b[...]).astype(BF16)
            return carry
        lax.fori_loop(0, count // chunk, body, 0, unroll=True)

    def values(count):
        def body(t, carry):
            start = pl.multiple_of(t * tile, tile)
            hv[:count, pl.ds(start, tile)] = dense(count, pl.ds(gate + start, tile))
            return carry
        lax.fori_loop(0, gate // tile, body, 0, unroll=True)

    chunk2 = 16

    def ln2(k, first, r):
        hs = pl.ds(pl.multiple_of(r * chunk2, chunk2), chunk2)
        ws = pl.ds(pl.multiple_of(block_of(k) * rows + first + r * chunk2, chunk2), chunk2)
        vn[ws, :] = layer_norm_rows(hv[hs, :].astype(F32), ln2s[...], ln2b[...]).astype(BF16)

    def ln2_all(k, first, count):
        def body(r, carry):
            ln2(k, first, r)
            return carry
        lax.fori_loop(0, count // chunk2, body, 0, unroll=True)

    def gates(k, first, count, with_ln2):
        per_tile = count // chunk2 // (gate // tile)
        gs = pl.ds(pl.multiple_of(first, count), count)

        def body(t, carry):
            cols = pl.ds(pl.multiple_of(t * tile, tile), tile)
            g[k, gs, cols] = dense(count, cols)
            if with_ln2:
                for r in range(per_tile):
                    ln2(k, first, t * per_tile + r)
            return carry
        lax.fori_loop(0, gate // tile, body, 0, unroll=True)

    def x_wait(k, half):
        rs = part_rows(half)
        pltpu.make_async_copy(xbuf.at[k, rs], xbuf.at[k, rs], xr_sem.at[k * HALVES + half]).wait()

    def do_own():
        for half in range(HALVES):
            x_wait(chip, half)
        for cp in smalls:
            cp.wait()
        ln1(chip, 0, rows)
        win_v.wait()
        for cp in spatial_loads:
            cp.start()
        values(rows)
        win_g.wait()
        wout_load.start()
        gates(chip, 0, rows, True)
        for half in range(HALVES):
            vn_copy(chip, half).start()

    def do_v(k, half):
        x_wait(k, half)
        first = half * part
        ln1(k, first, part)
        values(part)
        last = jnp.logical_and(k == (chip + chips // 2) % chips, half == HALVES - 1)

        @pl.when(last)
        def _():
            ln2_all(k, first, part)
            vn_copy(k, half).start()

        @pl.when(jnp.logical_not(last))
        def _():
            gates(k, first, part, True)
            vn_copy(k, half).start()

    def do_mask():
        for cp in spatial_loads:
            cp.wait()
        chunk = 32
        for k in range(chips):
            cols = slice(0, (k + 1) * cores * rows)

            def body(r, carry):
                rs = pl.ds(pl.multiple_of(r * chunk, chunk), chunk)
                keep = mask[k, rs, cols] > 0
                wm[k, rs, cols] = jnp.where(keep, wm[k, rs, cols].astype(F32), 0.0).astype(BF16)
                return carry
            lax.fori_loop(0, rows // chunk, body, 0)
        wout_load.wait()

    def out_copy(k, half):
        rs = part_rows(half)
        return pltpu.make_async_remote_copy(
            src_ref=obuf.at[k, rs], dst_ref=out_ref.at[chip, rs], send_sem=os_sem.at[k * HALVES + half],
            recv_sem=or_sem.at[chip * HALVES + half], device_id=(data, k * cores + core), device_id_type=MESH)

    def do_o(k, half):
        rs = part_rows(half)
        bias_row = bsp[:, pl.ds(pl.multiple_of(block_of(k) * rows + half * part, part), part)]
        bias = jnp.transpose(jnp.broadcast_to(bias_row, (128, part)))[:, :1]
        for kk in range(chips):
            @pl.when(k == kk)
            def _():
                depth = (kk + 1) * cores * rows

                def body(t, carry):
                    cols = pl.ds(pl.multiple_of(t * tile, tile), tile)
                    s = jnp.dot(wm[kk, rs, :depth], vn[:depth, cols], preferred_element_type=F32) + bias
                    q[:, cols] = (g[kk, rs, cols].astype(F32) * s.astype(BF16).astype(F32)).astype(BF16)
                    return carry
                lax.fori_loop(0, gate // tile, body, 0, unroll=True)
        out_tile = width // 2

        def out_body(t, carry):
            cols = pl.ds(pl.multiple_of(t * out_tile, out_tile), out_tile)
            y = jnp.dot(q[...], wout[:, cols], preferred_element_type=F32) + bout[:, cols]
            obuf[k, rs, cols] = (xbuf[k, rs, cols].astype(F32) + y).astype(BF16)
            return carry
        lax.fori_loop(0, width // out_tile, out_body, 0, unroll=True)

        @pl.when(k == chip)
        def _():
            pltpu.make_async_copy(obuf.at[k, rs], out_ref.at[chip, rs], or_sem.at[chip * HALVES + half]).start()

        @pl.when(k != chip)
        def _():
            out_copy(k, half).start()

    length = len(SCHEDULES[0])
    words = []
    for first in range(0, length, PER_WORD):
        word = jnp.int32(0)
        for c, steps in enumerate(SCHEDULES):
            word = jnp.where(chip == c, pack(steps[first:first + PER_WORD]), word)
        words.append(word)

    def step(i, carry):
        code = words[0]
        for n in range(1, len(words)):
            code = jnp.where(i >= n * PER_WORD, words[n], code)
        action = lax.shift_right_logical(code, BITS * (i % PER_WORD)) % (1 << BITS)

        @pl.when(action < W)
        def _():
            do_v(action // HALVES, action % HALVES)

        @pl.when(jnp.logical_and(action >= W, action < O_FIRST))
        def _():
            for half in range(HALVES):
                vn_copy(action - W, half).wait_recv()

        @pl.when(jnp.logical_and(action >= O_FIRST, action < G))
        def _():
            do_o((action - O_FIRST) // HALVES, action % HALVES)

        @pl.when(action == G)
        def _():
            gates((chip + chips // 2) % chips, (HALVES - 1) * part, part, False)
        return carry
    do_own()
    do_mask()
    lax.fori_loop(0, length, step, 0)

    for d in range(1, chips):
        for half in range(HALVES):
            x_copy(d, half).wait_send()
    for k in range(chips):
        for half in range(HALVES):
            vn_copy(k, half).wait_send()

        @pl.when(k != chip)
        def _():
            for half in range(HALVES):
                out_copy(k, half).wait_send()
    for k in range(chips):
        for half in range(HALVES):
            rs = part_rows(half)
            pltpu.make_async_copy(out_ref.at[k, rs], out_ref.at[k, rs], or_sem.at[k * HALVES + half]).wait()


def settle(src, dst, buf, in_sem, out_sem):
    count = src.shape[0]
    loads = [pltpu.make_async_copy(src.at[i], buf.at[i], in_sem.at[i]) for i in range(count)]
    stores = [pltpu.make_async_copy(buf.at[i], dst.at[i], out_sem.at[i]) for i in range(count)]
    for cp in loads:
        cp.start()
    for load, store in zip(loads, stores):
        load.wait()
        store.start()
    for cp in stores:
        cp.wait()


def solution(mesh):
    row_spec = P('data', 'seq', None)
    replicated = P()

    def local_block(act_in, ln1_scale, ln1_bias, w_in, b_in, ln2_scale, ln2_bias, w_spatial, b_spatial, causal_mask, w_out, b_out):
        chips, rows, width = act_in.shape
        cores = mesh.shape['seq'] // chips
        ffn, gate, total = w_in.shape[1], w_out.shape[0], w_spatial.shape[0]
        any_spec = pl.BlockSpec(memory_space=pl.ANY)
        row = lambda a: a.reshape(1, -1)
        dma = pltpu.SemaphoreType.DMA
        placed = pl.pallas_call(
            functools.partial(kernel, cores),
            out_shape=jax.ShapeDtypeStruct(act_in.shape, act_in.dtype),
            in_specs=[any_spec] * 12,
            out_specs=any_spec,
            scratch_shapes=[
                pltpu.VMEM((chips, rows, width), BF16),
                pltpu.VMEM((rows, width), BF16),
                pltpu.VMEM((rows, gate), BF16),
                pltpu.VMEM((chips, rows, gate), BF16),
                pltpu.VMEM((total, gate), BF16),
                pltpu.VMEM((chips, rows, total), BF16),
                pltpu.VMEM((chips, rows, total), jnp.int32),
                pltpu.VMEM((width, ffn), BF16),
                pltpu.VMEM((gate, width), BF16),
                pltpu.VMEM((rows // HALVES, gate), BF16),
                pltpu.VMEM((chips, rows, width), BF16),
                pltpu.VMEM((1, width), F32),
                pltpu.VMEM((1, width), F32),
                pltpu.VMEM((1, ffn), F32),
                pltpu.VMEM((1, gate), F32),
                pltpu.VMEM((1, gate), F32),
                pltpu.VMEM((1, total), F32),
                pltpu.VMEM((1, width), F32),
                dma((7,)), dma((2,)), dma, dma((chips,)), dma((chips,)),
                dma(((chips - 1) * HALVES,)), dma((chips * HALVES,)), dma((chips * HALVES,)), dma((chips * HALVES,)), dma((chips * HALVES,)), dma((chips * HALVES,)),
            ],
            compiler_params=pltpu.CompilerParams(collective_id=0, has_side_effects=True, vmem_limit_bytes=66_000_000),
        )(act_in, row(ln1_scale), row(ln1_bias), w_in, row(b_in), row(ln2_scale), row(ln2_bias), w_spatial, row(b_spatial),
          causal_mask, w_out, row(b_out))
        pieces = chips * HALVES
        piece = (pieces, rows // HALVES, width)
        return pl.pallas_call(
            settle,
            out_shape=jax.ShapeDtypeStruct(piece, act_in.dtype),
            in_specs=[any_spec],
            out_specs=any_spec,
            scratch_shapes=[pltpu.VMEM(piece, BF16), dma((pieces,)), dma((pieces,))],
        )(placed.reshape(piece)).reshape(act_in.shape)

    return jax.shard_map(local_block, mesh=mesh, in_specs=(row_spec,) + (replicated,) * 11, out_specs=row_spec, check_vma=False)
```

time: 67.4 us -> 60.2 us (0.89)
  the two profiles are of different devices: /device:TPU:112 before, /device:TPU:113 now
where the time goes in v3:
time: 60.2 us; the launch traced here: 60.1 us
  Pallas kernels  60.1 us (100%)
    pallas_call x1, Pallas kernels, local_block(): pl.pallas_call(functools.partial(kernel, cores), out_shape=jax.ShapeDtype...  57.7 us
    pallas_call x1, Pallas kernels, local_block(): pl.pallas_call(settle, out_shape=jax.ShapeDtypeStruct(piece, act_in.dtype...  2.39 us

profile of v3, /device:TPU:113, one launch (start us, length us, event | category | flops | bytes accessed | tf_op | source)
XLA Modules:
  0.0 60.1 jit_solution(11684769377825432192)
XLA Ops:
  0.0 57.7 %shard_map.118 = bf16[4,256,1024]{2,1,0:T(8,128)(2,1)} custom-call(bf16[4,256,1024]{2,1,0:T(8,128)(2,1)} %x_ref.1, f32[1,1024]{1,0:T(1,128)} %bitcast.14, f32[1,1024]{1,0:T(1,128)} %bitcast.15, bf16[1024,4096]{1,0:T(8,128)(2,1)} %win_h.1, f32[1,4096]{1,0:T(1,128)} %bitcast.10, f32[1,2048]{1,0:T(1,128)} %bitcast.11, f32[1,2048]{1,0:T(1,128)} %bitcast.12, ...), custom_call_target="tpu_custom_call" | custom-call | tf_op jit(solution)/shard_map/pallas_call | solution.py:337
  57.7 2.4 %shard_map.119 = bf16[8,128,1024]{2,1,0:T(8,128)(2,1)} custom-call(bf16[8,128,1024]{2,1,0:T(8,128)(2,1)} %bitcast.9), custom_call_target="tpu_custom_call" | custom-call | tf_op jit(solution)/shard_map/pallas_call | solution.py:369

commit v4 on v3

--- a/solution.py
+++ b/solution.py
@@ -13,6 +13,7 @@
 BF16 = jnp.bfloat16
 
 HALVES = 2
+PIECES = 3
 
 
 def V(k, half):
@@ -23,17 +24,23 @@
     return 12 + k * HALVES + half
 
 
-W, O_FIRST, G, BITS, PER_WORD = 8, 12, 20, 5, 6
+W, O_FIRST, G, PART, LEAD, BITS, PER_WORD = 8, 12, 20, 21, 22, 5, 6
 SCHEDULES = (
-    (V(1, 0), V(3, 0), V(1, 1), V(3, 1), V(2, 0), W + 0, W + 1, O(1, 0), O(1, 1), V(2, 1), W + 2, W + 3,
-     O(3, 0), O(3, 1), G, O(2, 0), O(2, 1), O(0, 0), O(0, 1)),
-    (V(0, 0), V(2, 0), V(0, 1), V(2, 1), W + 0, W + 1, O(0, 0), O(0, 1), V(3, 0), W + 2, O(2, 0), O(2, 1), V(3, 1), W + 3,
-     O(3, 0), G, O(3, 1), O(1, 0), O(1, 1)),
-    (V(1, 0), V(3, 0), V(1, 1), V(3, 1), V(0, 0), V(0, 1), W + 0, W + 1, O(1, 0), O(0, 0), O(1, 1), G, O(0, 1), W + 2, W + 3,
+    (V(1, 0), V(3, 0), V(1, 1), V(3, 1), V(2, 0), W + 0, W + 1, O(1, 0), V(2, 1), W + 3, PART, W + 2, LEAD,
+     O(3, 1), O(1, 1), G, O(2, 0), O(2, 1), O(0, 0), O(0, 1)),
+) * 2 + (
+    (V(0, 0), V(2, 0), V(0, 1), V(2, 1), W + 0, W + 1, O(0, 0), O(0, 1), V(3, 0), W + 2, O(2, 0), O(2, 1), V(3, 1), PART, W + 3, LEAD,
+     G, O(3, 1), O(1, 0), O(1, 1)),
+) * 2 + (
+    (V(1, 0), V(3, 0), V(1, 1), V(3, 1), V(0, 0), W + 1, PART, V(0, 1), G, W + 0, LEAD, O(0, 0), O(1, 1), O(0, 1), W + 2, W + 3,
      O(3, 0), O(3, 1), O(2, 0), O(2, 1)),
-    (V(0, 0), V(2, 0), V(0, 1), V(2, 1), W + 0, O(0, 0), O(0, 1), V(1, 0), V(1, 1), W + 1, O(1, 0), W + 2, O(2, 0), G,
+    (V(1, 0), V(3, 0), V(1, 1), V(3, 1), V(0, 0), W + 1, PART, V(0, 1), G, W + 0, O(0, 0), LEAD, O(0, 1), O(1, 1), W + 2, W + 3,
+     O(3, 0), O(3, 1), O(2, 0), O(2, 1)),
+) + (
+    (V(0, 0), V(2, 0), V(0, 1), V(2, 1), W + 0, O(0, 0), O(0, 1), V(1, 0), PART, V(1, 1), G, W + 1, LEAD, W + 2, O(2, 0),
      O(1, 1), O(2, 1), W + 3, O(3, 0), O(3, 1)),
-)
+) * 2
+LEADS = ((3, ((0, 2), (3, 4)), True), (3, ((0, 3),), True), (1, ((1, 2),), False), (1, ((0, 1),), False))
 
 
 def pack(steps):
@@ -54,21 +61,28 @@
 
 
 def kernel(cores, x_ref, ln1s_h, ln1b_h, win_h, bin_h, ln2s_h, ln2b_h, wsp_h, bsp_h, mask_h, wout_h, bout_h, out_ref,
-           xbuf, u, hv, g, vn, wm, mask, win, wout, q, obuf, ln1s, ln1b, b_in, ln2s, ln2b, bsp, bout,
+           xbuf, u, hv, g, vn, wm, mask, win, wout, q, acc, obuf, ln1s, ln1b, b_in, ln2s, ln2b, bsp, bout,
            small_sem, win_sem, wout_sem, wsp_sem, mask_sem, xs_sem, xr_sem, vs_sem, vr_sem, os_sem, or_sem):
     data, me = lax.axis_index("data"), lax.axis_index("seq")
     chip, core = me // cores, me % cores
-    partner = (data, chip * cores + (cores - 1 - core))
+    other = cores - 1 - core
+    partner = (data, chip * cores + other)
     chips, rows, width = x_ref.shape
     gate = wout_h.shape[0]
 
     def block_of(k):
-        return k * cores + core
+        return k * cores + jnp.where(k == chip, core, other)
 
     def row_slice(k):
         return pl.ds(pl.multiple_of(block_of(k) * rows, rows), rows)
 
+    barrier = pltpu.get_barrier_semaphore()
+    for d in range(1, chips):
+        pl.semaphore_signal(barrier, inc=1, device_id=(data, (chip + d) % chips * cores + other), device_id_type=MESH)
+    pl.semaphore_signal(barrier, inc=1, device_id=partner, device_id_type=MESH)
+
     part = rows // HALVES
+    far = (chip + chips // 2) % chips
 
     def part_rows(half):
         return pl.ds(pl.multiple_of(half * part, part), part)
@@ -85,10 +99,6 @@
     win_v.start()
     win_g.start()
 
-    barrier = pltpu.get_barrier_semaphore()
-    pl.semaphore_signal(barrier, inc=1, device_id=partner, device_id_type=MESH)
-    for d in range(1, chips):
-        pl.semaphore_signal(barrier, inc=1, device_id=(data, (chip + d) % chips * cores + core), device_id_type=MESH)
     pl.semaphore_wait(barrier, chips)
 
     def x_copy(d, half):
@@ -96,7 +106,7 @@
         rs = part_rows(half)
         return pltpu.make_async_remote_copy(
             src_ref=x_ref.at[to, rs], dst_ref=xbuf.at[chip, rs], send_sem=xs_sem.at[(d - 1) * HALVES + half],
-            recv_sem=xr_sem.at[chip * HALVES + half], device_id=(data, to * cores + core), device_id_type=MESH)
+            recv_sem=xr_sem.at[chip * HALVES + half], device_id=(data, to * cores + other), device_id_type=MESH)
 
     near = [d for d in range(1, chips) if d != chips // 2]
     for group in (near, [chips // 2]):
@@ -119,11 +129,26 @@
         a = jnp.dot(u[:count, :], win[:, cols], preferred_element_type=F32) + b_in[:, cols]
         return gelu(a).astype(BF16)
 
-    def vn_copy(k, half):
-        ws = pl.ds(pl.multiple_of(block_of(k) * rows + half * part, part), part)
+    def vn_copy(k, first, count, i):
+        ws = pl.ds(pl.multiple_of(block_of(k) * rows + first, count), count)
         return pltpu.make_async_remote_copy(
-            src_ref=vn.at[ws, :], dst_ref=vn.at[ws, :], send_sem=vs_sem.at[k * HALVES + half],
-            recv_sem=vr_sem.at[k * HALVES + half], device_id=partner, device_id_type=MESH)
+            src_ref=vn.at[ws, :], dst_ref=vn.at[ws, :], send_sem=vs_sem.at[k * PIECES + i],
+            recv_sem=vr_sem.at[k * PIECES + i], device_id=partner, device_id_type=MESH)
+
+    def last_vn(i):
+        return vn_copy(far, part + i * (part // 2), part // 2, 1 + i)
+
+    def each_vn_copy(k, act):
+        act(vn_copy(k, 0, part, 0))
+
+        @pl.when(k != far)
+        def _():
+            act(vn_copy(k, part, part, 1))
+
+        @pl.when(k == far)
+        def _():
+            for i in range(2):
+                act(last_vn(i))
 
     def ln1(k, first, count):
         chunk = 32
@@ -149,11 +174,14 @@
         ws = pl.ds(pl.multiple_of(block_of(k) * rows + first + r * chunk2, chunk2), chunk2)
         vn[ws, :] = layer_norm_rows(hv[hs, :].astype(F32), ln2s[...], ln2b[...]).astype(BF16)
 
-    def ln2_all(k, first, count):
-        def body(r, carry):
-            ln2(k, first, r)
-            return carry
-        lax.fori_loop(0, count // chunk2, body, 0, unroll=True)
+    def ln2_last():
+        each = part // 2 // chunk2
+        for i in range(2):
+            def body(r, carry):
+                ln2(far, part, i * each + r)
+                return carry
+            lax.fori_loop(0, each, body, 0, unroll=True)
+            last_vn(i).start()
 
     def gates(k, first, count, with_ln2):
         per_tile = count // chunk2 // (gate // tile)
@@ -185,25 +213,26 @@
         win_g.wait()
         wout_load.start()
         gates(chip, 0, rows, True)
-        for half in range(HALVES):
-            vn_copy(chip, half).start()
+        each_vn_copy(chip, lambda cp: cp.start())
 
     def do_v(k, half):
         x_wait(k, half)
         first = half * part
         ln1(k, first, part)
         values(part)
-        last = jnp.logical_and(k == (chip + chips // 2) % chips, half == HALVES - 1)
+        last = jnp.logical_and(k == far, half == HALVES - 1)
 
         @pl.when(last)
         def _():
-            ln2_all(k, first, part)
-            vn_copy(k, half).start()
+            ln2_last()
 
         @pl.when(jnp.logical_not(last))
         def _():
             gates(k, first, part, True)
-            vn_copy(k, half).start()
+            for which in range(HALVES):
+                @pl.when(half == which)
+                def _():
+                    vn_copy(k, which * part, part, which).start()
 
     def do_mask():
         for cp in spatial_loads:
@@ -224,23 +253,70 @@
         rs = part_rows(half)
         return pltpu.make_async_remote_copy(
             src_ref=obuf.at[k, rs], dst_ref=out_ref.at[chip, rs], send_sem=os_sem.at[k * HALVES + half],
-            recv_sem=or_sem.at[chip * HALVES + half], device_id=(data, k * cores + core), device_id_type=MESH)
+            recv_sem=or_sem.at[chip * HALVES + half], device_id=(data, k * cores + other), device_id_type=MESH)
+
+    def bias_of(k, half):
+        bias_row = bsp[:, pl.ds(pl.multiple_of(block_of(k) * rows + half * part, part), part)]
+        return jnp.transpose(jnp.broadcast_to(bias_row, (128, part)))[:, :1]
+
+    def over_tiles(body):
+        def step(t, carry):
+            body(pl.ds(pl.multiple_of(t * tile, tile), tile))
+            return carry
+        lax.fori_loop(0, gate // tile, step, 0, unroll=True)
+
+    def gated(k, rs, cols, s):
+        return (g[k, rs, cols].astype(F32) * s.astype(BF16).astype(F32)).astype(BF16)
 
     def do_o(k, half):
         rs = part_rows(half)
-        bias_row = bsp[:, pl.ds(pl.multiple_of(block_of(k) * rows + half * part, part), part)]
-        bias = jnp.transpose(jnp.broadcast_to(bias_row, (128, part)))[:, :1]
+        bias = bias_of(k, half)
         for kk in range(chips):
             @pl.when(k == kk)
             def _():
                 depth = (kk + 1) * cores * rows
 
-                def body(t, carry):
-                    cols = pl.ds(pl.multiple_of(t * tile, tile), tile)
+                def body(cols):
                     s = jnp.dot(wm[kk, rs, :depth], vn[:depth, cols], preferred_element_type=F32) + bias
-                    q[:, cols] = (g[kk, rs, cols].astype(F32) * s.astype(BF16).astype(F32)).astype(BF16)
-                    return carry
-                lax.fori_loop(0, gate // tile, body, 0, unroll=True)
+                    q[:, cols] = gated(kk, rs, cols, s)
+                over_tiles(body)
+        finish_o(k, half)
+
+    def do_part():
+        own_block = pl.ds(pl.multiple_of((far * cores + other) * rows, rows), rows)
+        for c, (k, spans, with_own) in enumerate(LEADS):
+            @pl.when(chip == c)
+            def _():
+                def body(cols):
+                    terms = [slice(first * cores * rows, end * cores * rows) for first, end in spans]
+                    if with_own:
+                        terms.append(own_block)
+                    acc[:, cols] = sum(
+                        jnp.dot(wm[k, :part, js], vn[js, cols], preferred_element_type=F32) for js in terms)
+                over_tiles(body)
+
+    def do_lead():
+        k = lead
+        bias = bias_of(k, 0)
+        rs = pl.ds(0, part)
+
+        def rest(js):
+            def body(cols):
+                s = jnp.dot(wm[k, rs, js], vn[js, cols], preferred_element_type=F32) + acc[:, cols] + bias
+                q[:, cols] = gated(k, rs, cols, s)
+            over_tiles(body)
+
+        @pl.when(had_own)
+        def _():
+            rest(pl.ds(pl.multiple_of((far * cores + core) * rows, rows), rows))
+
+        @pl.when(jnp.logical_not(had_own))
+        def _():
+            rest(pl.ds(pl.multiple_of(far * cores * rows, cores * rows), cores * rows))
+        finish_o(k, 0)
+
+    def finish_o(k, half):
+        rs = part_rows(half)
         out_tile = width // 2
 
         def out_body(t, carry):
@@ -258,12 +334,16 @@
         def _():
             out_copy(k, half).start()
 
+    lead, had_own = jnp.int32(0), False
+    for c, (k, _, with_own) in enumerate(LEADS):
+        lead = jnp.where(chip == c, k, lead)
+        had_own = jnp.logical_or(had_own, jnp.logical_and(chip == c, with_own))
     length = len(SCHEDULES[0])
     words = []
     for first in range(0, length, PER_WORD):
         word = jnp.int32(0)
         for c, steps in enumerate(SCHEDULES):
-            word = jnp.where(chip == c, pack(steps[first:first + PER_WORD]), word)
+            word = jnp.where(me == c, pack(steps[first:first + PER_WORD]), word)
         words.append(word)
 
     def step(i, carry):
@@ -278,8 +358,7 @@
 
         @pl.when(jnp.logical_and(action >= W, action < O_FIRST))
         def _():
-            for half in range(HALVES):
-                vn_copy(action - W, half).wait_recv()
+            each_vn_copy(action - W, lambda cp: cp.wait_recv())
 
         @pl.when(jnp.logical_and(action >= O_FIRST, action < G))
         def _():
@@ -287,7 +366,15 @@
 
         @pl.when(action == G)
         def _():
-            gates((chip + chips // 2) % chips, (HALVES - 1) * part, part, False)
+            gates(far, (HALVES - 1) * part, part, False)
+
+        @pl.when(action == PART)
+        def _():
+            do_part()
+
+        @pl.when(action == LEAD)
+        def _():
+            do_lead()
         return carry
     do_own()
     do_mask()
@@ -297,8 +384,7 @@
         for half in range(HALVES):
             x_copy(d, half).wait_send()
     for k in range(chips):
-        for half in range(HALVES):
-            vn_copy(k, half).wait_send()
+        each_vn_copy(k, lambda cp: cp.wait_send())
 
         @pl.when(k != chip)
         def _():
@@ -308,19 +394,6 @@
         for half in range(HALVES):
             rs = part_rows(half)
             pltpu.make_async_copy(out_ref.at[k, rs], out_ref.at[k, rs], or_sem.at[k * HALVES + half]).wait()
-
-
-def settle(src, dst, buf, in_sem, out_sem):
-    count = src.shape[0]
-    loads = [pltpu.make_async_copy(src.at[i], buf.at[i], in_sem.at[i]) for i in range(count)]
-    stores = [pltpu.make_async_copy(buf.at[i], dst.at[i], out_sem.at[i]) for i in range(count)]
-    for cp in loads:
-        cp.start()
-    for load, store in zip(loads, stores):
-        load.wait()
-        store.start()
-    for cp in stores:
-        cp.wait()
 
 
 def solution(mesh):
@@ -334,11 +407,11 @@
         any_spec = pl.BlockSpec(memory_space=pl.ANY)
         row = lambda a: a.reshape(1, -1)
         dma = pltpu.SemaphoreType.DMA
-        placed = pl.pallas_call(
+        return pl.pallas_call(
             functools.partial(kernel, cores),
-            out_shape=jax.ShapeDtypeStruct(act_in.shape, act_in.dtype),
+            out_shape=pltpu.VMEM(act_in.shape, act_in.dtype),
             in_specs=[any_spec] * 12,
-            out_specs=any_spec,
+            out_specs=pl.BlockSpec(memory_space=pltpu.VMEM),
             scratch_shapes=[
                 pltpu.VMEM((chips, rows, width), BF16),
                 pltpu.VMEM((rows, width), BF16),
@@ -350,6 +423,7 @@
                 pltpu.VMEM((width, ffn), BF16),
                 pltpu.VMEM((gate, width), BF16),
                 pltpu.VMEM((rows // HALVES, gate), BF16),
+                pltpu.VMEM((rows // HALVES, gate), F32),
                 pltpu.VMEM((chips, rows, width), BF16),
                 pltpu.VMEM((1, width), F32),
                 pltpu.VMEM((1, width), F32),
@@ -359,19 +433,10 @@
                 pltpu.VMEM((1, total), F32),
                 pltpu.VMEM((1, width), F32),
                 dma((7,)), dma((2,)), dma, dma((chips,)), dma((chips,)),
-                dma(((chips - 1) * HALVES,)), dma((chips * HALVES,)), dma((chips * HALVES,)), dma((chips * HALVES,)), dma((chips * HALVES,)), dma((chips * HALVES,)),
+                dma(((chips - 1) * HALVES,)), dma((chips * HALVES,)), dma((chips * PIECES,)), dma((chips * PIECES,)), dma((chips * HALVES,)), dma((chips * HALVES,)),
             ],
-            compiler_params=pltpu.CompilerParams(collective_id=0, has_side_effects=True, vmem_limit_bytes=66_000_000),
+            compiler_params=pltpu.CompilerParams(collective_id=0, has_side_effects=True, vmem_limit_bytes=60_000_000),
         )(act_in, row(ln1_scale), row(ln1_bias), w_in, row(b_in), row(ln2_scale), row(ln2_bias), w_spatial, row(b_spatial),
           causal_mask, w_out, row(b_out))
-        pieces = chips * HALVES
-        piece = (pieces, rows // HALVES, width)
-        return pl.pallas_call(
-            settle,
-            out_shape=jax.ShapeDtypeStruct(piece, act_in.dtype),
-            in_specs=[any_spec],
-            out_specs=any_spec,
-            scratch_shapes=[pltpu.VMEM(piece, BF16), dma((pieces,)), dma((pieces,))],
-        )(placed.reshape(piece)).reshape(act_in.shape)
 
     return jax.shard_map(local_block, mesh=mesh, in_specs=(row_spec,) + (replicated,) * 11, out_specs=row_spec, check_vma=False)

time: 60.2 us -> 58.7 us (0.975)
  the two profiles are of different devices: /device:TPU:113 before, /device:TPU:112 now
where the time goes in v4:
time: 58.7 us; the launch traced here: 58 us
  Pallas kernels  56.7 us (97%)
  local copies, waits for them, and re-layouts  1.32 us (2%)
    pallas_call x1, Pallas kernels, local_block(): pl.pallas_call(functools.partial(kernel, cores), out_shape=pltpu.VMEM(act...  56.7 us
    unnamed x1, local copies, waits for them, and re-layouts  1.32 us

profile of v4, /device:TPU:112, one launch (start us, length us, event | category | flops | bytes accessed | tf_op | source)
XLA Modules:
  0.0 58.0 jit_solution(6546658632347088692)
XLA Ops:
  0.0 56.7 %shard_map.118 = bf16[4,256,1024]{2,1,0:T(8,128)(2,1)S(1)} custom-call(bf16[4,256,1024]{2,1,0:T(8,128)(2,1)} %x_ref.1, f32[1,1024]{1,0:T(1,128)} %bitcast.11, f32[1,1024]{1,0:T(1,128)} %bitcast.12, bf16[1024,4096]{1,0:T(8,128)(2,1)} %win_h.1, f32[1,4096]{1,0:T(1,128)} %bitcast.7, f32[1,2048]{1,0:T(1,128)} %bitcast.8, f32[1,2048]{1,0:T(1,128)} %bitcast.9, ...), custom_call_target="tpu_custom_call" | custom-call | tf_op jit(solution)/shard_map/pallas_call | solution.py:410
  56.7 1.3 %copy.14 = bf16[4,256,1024]{2,1,0:T(8,128)(2,1)} copy(bf16[4,256,1024]{2,1,0:T(8,128)(2,1)S(1)} %shard_map.118) | data formatting | bytes 4194304

commit v5 on v4

--- a/solution.py
+++ b/solution.py
@@ -24,27 +24,27 @@
     return 12 + k * HALVES + half
 
 
-W, O_FIRST, G, PART, LEAD, BITS, PER_WORD = 8, 12, 20, 21, 22, 5, 6
+W, O_FIRST, G, PART, LEAD, OWN, LAST, NONE, BITS, PER_WORD = 8, 12, 20, 21, 22, 23, 24, 31, 5, 6
 SCHEDULES = (
-    (V(1, 0), V(3, 0), V(1, 1), V(3, 1), V(2, 0), W + 0, W + 1, O(1, 0), V(2, 1), W + 3, PART, W + 2, LEAD,
+    (V(1, 0), V(3, 0), V(1, 1), V(3, 1), V(2, 0), W + 0, W + 1, O(1, 0), LAST, W + 3, PART, W + 2, LEAD,
      O(3, 1), O(1, 1), G, O(2, 0), O(2, 1), O(0, 0), O(0, 1)),
 ) * 2 + (
-    (V(0, 0), V(2, 0), V(0, 1), V(2, 1), W + 0, W + 1, O(0, 0), O(0, 1), V(3, 0), W + 2, O(2, 0), O(2, 1), V(3, 1), PART, W + 3, LEAD,
+    (V(0, 0), V(2, 0), V(0, 1), V(2, 1), W + 0, W + 1, O(0, 0), O(0, 1), V(3, 0), W + 2, O(2, 0), O(2, 1), LAST, PART, W + 3, LEAD,
      G, O(3, 1), O(1, 0), O(1, 1)),
 ) * 2 + (
-    (V(1, 0), V(3, 0), V(1, 1), V(3, 1), V(0, 0), W + 1, PART, V(0, 1), G, W + 0, LEAD, O(0, 0), O(1, 1), O(0, 1), W + 2, W + 3,
+    (V(1, 0), V(3, 0), V(1, 1), V(3, 1), V(0, 0), W + 1, PART, LAST, G, OWN, W + 0, LEAD, O(0, 0), O(1, 1), O(0, 1), W + 2, W + 3,
      O(3, 0), O(3, 1), O(2, 0), O(2, 1)),
-    (V(1, 0), V(3, 0), V(1, 1), V(3, 1), V(0, 0), W + 1, PART, V(0, 1), G, W + 0, O(0, 0), LEAD, O(0, 1), O(1, 1), W + 2, W + 3,
+    (V(1, 0), V(3, 0), V(1, 1), V(3, 1), V(0, 0), W + 1, PART, LAST, G, OWN, W + 0, O(0, 0), LEAD, O(0, 1), O(1, 1), W + 2, W + 3,
      O(3, 0), O(3, 1), O(2, 0), O(2, 1)),
 ) + (
-    (V(0, 0), V(2, 0), V(0, 1), V(2, 1), W + 0, O(0, 0), O(0, 1), V(1, 0), PART, V(1, 1), G, W + 1, LEAD, W + 2, O(2, 0),
+    (V(0, 0), V(2, 0), V(0, 1), V(2, 1), W + 0, O(0, 0), O(0, 1), V(1, 0), PART, LAST, G, OWN, W + 1, LEAD, W + 2, O(2, 0),
      O(1, 1), O(2, 1), W + 3, O(3, 0), O(3, 1)),
 ) * 2
 LEADS = ((3, ((0, 2), (3, 4)), True), (3, ((0, 3),), True), (1, ((1, 2),), False), (1, ((0, 1),), False))
 
 
 def pack(steps):
-    return sum(s << (BITS * i) for i, s in enumerate(steps))
+    return sum(steps[i] << (BITS * i) if i < len(steps) else NONE << (BITS * i) for i in range(PER_WORD))
 
 
 def layer_norm_rows(rows, gain, shift):
@@ -220,19 +220,17 @@
         first = half * part
         ln1(k, first, part)
         values(part)
-        last = jnp.logical_and(k == far, half == HALVES - 1)
-
-        @pl.when(last)
-        def _():
-            ln2_last()
-
-        @pl.when(jnp.logical_not(last))
-        def _():
-            gates(k, first, part, True)
-            for which in range(HALVES):
-                @pl.when(half == which)
-                def _():
-                    vn_copy(k, which * part, part, which).start()
+        gates(k, first, part, True)
+        for which in range(HALVES):
+            @pl.when(half == which)
+            def _():
+                vn_copy(k, which * part, part, which).start()
+
+    def do_last():
+        x_wait(far, HALVES - 1)
+        ln1(far, part, part)
+        values(part)
+        ln2_last()
 
     def do_mask():
         for cp in spatial_loads:
@@ -300,20 +298,20 @@
         bias = bias_of(k, 0)
         rs = pl.ds(0, part)
 
-        def rest(js):
-            def body(cols):
-                s = jnp.dot(wm[k, rs, js], vn[js, cols], preferred_element_type=F32) + acc[:, cols] + bias
-                q[:, cols] = gated(k, rs, cols, s)
-            over_tiles(body)
-
-        @pl.when(had_own)
-        def _():
-            rest(pl.ds(pl.multiple_of((far * cores + core) * rows, rows), rows))
-
-        @pl.when(jnp.logical_not(had_own))
-        def _():
-            rest(pl.ds(pl.multiple_of(far * cores * rows, cores * rows), cores * rows))
+        last_block = pl.ds(pl.multiple_of((far * cores + core) * rows, rows), rows)
+
+        def body(cols):
+            s = jnp.dot(wm[k, rs, last_block], vn[last_block, cols], preferred_element_type=F32) + acc[:, cols] + bias
+            q[:, cols] = gated(k, rs, cols, s)
+        over_tiles(body)
         finish_o(k, 0)
+
+    def do_own_term():
+        own_block = pl.ds(pl.multiple_of((far * cores + other) * rows, rows), rows)
+
+        def body(cols):
+            acc[:, cols] += jnp.dot(wm[lead, :part, own_block], vn[own_block, cols], preferred_element_type=F32)
+        over_tiles(body)
 
     def finish_o(k, half):
         rs = part_rows(half)
@@ -334,11 +332,10 @@
         def _():
             out_copy(k, half).start()
 
-    lead, had_own = jnp.int32(0), False
-    for c, (k, _, with_own) in enumerate(LEADS):
+    lead = jnp.int32(0)
+    for c, (k, _, _) in enumerate(LEADS):
         lead = jnp.where(chip == c, k, lead)
-        had_own = jnp.logical_or(had_own, jnp.logical_and(chip == c, with_own))
-    length = len(SCHEDULES[0])
+    length = max(len(steps) for steps in SCHEDULES)
     words = []
     for first in range(0, length, PER_WORD):
         word = jnp.int32(0)
@@ -375,6 +372,14 @@
         @pl.when(action == LEAD)
         def _():
             do_lead()
+
+        @pl.when(action == OWN)
+        def _():
+            do_own_term()
+
+        @pl.when(action == LAST)
+        def _():
+            do_last()
         return carry
     do_own()
     do_mask()

time: 58.7 us -> 58.5 us (level)
  no operation moved by 1% of the time
where the time goes in v5:
time: 58.5 us; the launch traced here: 57.7 us
  Pallas kernels  56.4 us (96%)
  local copies, waits for them, and re-layouts  1.32 us (2%)
    pallas_call x1, Pallas kernels, local_block(): pl.pallas_call(functools.partial(kernel, cores), out_shape=pltpu.VMEM(act...  56.4 us
    unnamed x1, local copies, waits for them, and re-layouts  1.32 us

profile of v5, /device:TPU:112, one launch (start us, length us, event | category | flops | bytes accessed | tf_op | source)
XLA Modules:
  0.0 57.7 jit_solution(13681296496810801989)
XLA Ops:
  0.0 56.4 %shard_map.118 = bf16[4,256,1024]{2,1,0:T(8,128)(2,1)S(1)} custom-call(bf16[4,256,1024]{2,1,0:T(8,128)(2,1)} %x_ref.1, f32[1,1024]{1,0:T(1,128)} %bitcast.11, f32[1,1024]{1,0:T(1,128)} %bitcast.12, bf16[1024,4096]{1,0:T(8,128)(2,1)} %win_h.1, f32[1,4096]{1,0:T(1,128)} %bitcast.7, f32[1,2048]{1,0:T(1,128)} %bitcast.8, f32[1,2048]{1,0:T(1,128)} %bitcast.9, ...), custom_call_target="tpu_custom_call" | custom-call | tf_op jit(solution)/shard_map/pallas_call | solution.py:415
  56.4 1.3 %copy.14 = bf16[4,256,1024]{2,1,0:T(8,128)(2,1)} copy(bf16[4,256,1024]{2,1,0:T(8,128)(2,1)S(1)} %shard_map.118) | data formatting | bytes 4194304

commit v6 on v5

--- a/solution.py
+++ b/solution.py
@@ -304,7 +304,13 @@
             s = jnp.dot(wm[k, rs, last_block], vn[last_block, cols], preferred_element_type=F32) + acc[:, cols] + bias
             q[:, cols] = gated(k, rs, cols, s)
         over_tiles(body)
-        finish_o(k, 0)
+        for t in range(2):
+            cs = slice(t * (width // 2), (t + 1) * (width // 2))
+            y = jnp.dot(q[...], wout[:, cs], preferred_element_type=F32) + bout[:, cs]
+            obuf[k, rs, cs] = (xbuf[k, rs, cs].astype(F32) + y).astype(BF16)
+            pltpu.make_async_remote_copy(
+                src_ref=obuf.at[k, rs, cs], dst_ref=out_ref.at[chip, rs, cs], send_sem=os_sem.at[k * HALVES],
+                recv_sem=or_sem.at[chip * HALVES], device_id=(data, k * cores + other), device_id_type=MESH).start()
 
     def do_own_term():
         own_block = pl.ds(pl.multiple_of((far * cores + other) * rows, rows), rows)

time: 58.5 us -> 58.2 us (level)
  no operation moved by 1% of the time
where the time goes in v6:
time: 58.2 us; the launch traced here: 57.5 us
  Pallas kernels  56.1 us (96%)
  local copies, waits for them, and re-layouts  1.32 us (2%)
    pallas_call x1, Pallas kernels, local_block(): pl.pallas_call(functools.partial(kernel, cores), out_shape=pltpu.VMEM(act...  56.1 us
    unnamed x1, local copies, waits for them, and re-layouts  1.32 us

profile of v6, /device:TPU:112, one launch (start us, length us, event | category | flops | bytes accessed | tf_op | source)
XLA Modules:
  0.0 57.5 jit_solution(3888379754633599325)
XLA Ops:
  0.0 56.1 %shard_map.118 = bf16[4,256,1024]{2,1,0:T(8,128)(2,1)S(1)} custom-call(bf16[4,256,1024]{2,1,0:T(8,128)(2,1)} %x_ref.1, f32[1,1024]{1,0:T(1,128)} %bitcast.11, f32[1,1024]{1,0:T(1,128)} %bitcast.12, bf16[1024,4096]{1,0:T(8,128)(2,1)} %win_h.1, f32[1,4096]{1,0:T(1,128)} %bitcast.7, f32[1,2048]{1,0:T(1,128)} %bitcast.8, f32[1,2048]{1,0:T(1,128)} %bitcast.9, ...), custom_call_target="tpu_custom_call" | custom-call | tf_op jit(solution)/shard_map/pallas_call | solution.py:421
  56.1 1.3 %copy.14 = bf16[4,256,1024]{2,1,0:T(8,128)(2,1)} copy(bf16[4,256,1024]{2,1,0:T(8,128)(2,1)S(1)} %shard_map.118) | data formatting | bytes 4194304
